TPU v7x, 32 devices: a 4x2x2 block of a 4x4x8 slice. The times are simulated.
32 devices in a mesh: dp: 4 (over y, z), cp: 8 (over x, core).
Axes of the slice: x: 4, y: 2, z: 2, core: 2. Of those that a mesh axis runs over, the one named last changes fastest.
The devices are a block of a 4x4x8 slice.
Arguments:
- q_tok: bfloat16 [16384, 7, 128], P(('dp', 'cp')), parts along dimension 0
- k_tok: bfloat16 [16384, 128], P(('dp', 'cp')), parts along dimension 0
- v_tok: bfloat16 [16384, 128], P(('dp', 'cp')), parts along dimension 0
- fwd_out: bfloat16 [16384, 7, 128], P(('dp', 'cp')), parts along dimension 0
- d_out: bfloat16 [16384, 7, 128], P(('dp', 'cp')), parts along dimension 0
- lse_row: float32 [16384, 7], P(('dp', 'cp')), parts along dimension 0
Outputs:
- output 1: bfloat16 [16384, 7, 128], P(('dp', 'cp')), parts along dimension 0
- output 2: bfloat16 [16384, 128], P(('dp', 'cp')), parts along dimension 0
- output 3: bfloat16 [16384, 128], P(('dp', 'cp')), parts along dimension 0
There are 4 independent parts. A program takes and returns all parts, laid end to end along the dimension named above; each array names one.
All inputs are finite; a program needn't handle non-finite values.
Results may differ from a plain program's by a relative error of at most 0.001.
Values are sent between devices in bfloat16 or wider.
A program may use at most 768 MiB of HBM per device.

v0:
```python
import jax
import jax.numpy as jnp
from jax import lax
from jax.sharding import PartitionSpec as P


def pair_scores(q_block, do_block, lse_block, delta_block, k_block, v_block, on_diag, softmax_scale):
    logits = jnp.einsum('rgd,cd->rgc', q_block, k_block, preferred_element_type=jnp.float32)
    row_ids = jnp.arange(q_block.shape[0])
    allowed = jnp.logical_or(row_ids[None, :] <= row_ids[:, None], jnp.logical_not(on_diag))
    prob_mat = jnp.exp(jnp.where(allowed[:, None, :], logits * softmax_scale - lse_block[:, :, None], -jnp.inf))
    d_prob = jnp.einsum('rgd,cd->rgc', do_block, v_block, preferred_element_type=jnp.float32)
    d_score = (prob_mat * (d_prob - delta_block[:, :, None])).astype(jnp.bfloat16)
    return prob_mat.astype(jnp.bfloat16), d_score


def solution(mesh):
    n_dev = mesh.shape['cp']
    forward_perm = [(i, (i + 1) % n_dev) for i in range(n_dev)]
    row_spec = P(('dp', 'cp'))

    def local_fn(q_tok, k_tok, v_tok, fwd_out, d_out, lse_row):
        softmax_scale = q_tok.shape[-1] ** -0.5
        my_index = lax.axis_index('cp')
        row_delta = jnp.einsum('rgd,rgd->rg', d_out, fwd_out, preferred_element_type=jnp.float32)

        def accumulate(step, state):
            def pair_update(state_in):
                dq_acc, k_cur, v_cur, dk_acc, dv_acc = state_in
                prob_low, score_low = pair_scores(q_tok, d_out, lse_row, row_delta, k_cur, v_cur, step == 0, softmax_scale)
                dq_acc = dq_acc + jnp.einsum('rgc,cd->rgd', score_low, k_cur, preferred_element_type=jnp.float32)
                dk_acc = dk_acc + jnp.einsum('rgc,rgd->cd', score_low, q_tok, preferred_element_type=jnp.float32)
                dv_acc = dv_acc + jnp.einsum('rgc,rgd->cd', prob_low, d_out, preferred_element_type=jnp.float32)
                return (dq_acc, k_cur, v_cur, dk_acc, dv_acc)

            def keep_state(state_in):
                return state_in

            return lax.cond(step <= my_index, pair_update, keep_state, state)

        def step_fn(step, state):
            dq_acc, k_cur, v_cur, dk_acc, dv_acc = accumulate(step, state)
            k_next = lax.ppermute(k_cur, 'cp', forward_perm)
            v_next = lax.ppermute(v_cur, 'cp', forward_perm)
            dk_next = lax.ppermute(dk_acc, 'cp', forward_perm)
            dv_next = lax.ppermute(dv_acc, 'cp', forward_perm)
            return (dq_acc, k_next, v_next, dk_next, dv_next)

        kv_zeros = jnp.zeros(k_tok.shape, jnp.float32)
        state = (jnp.zeros(q_tok.shape, jnp.float32), k_tok, v_tok, kv_zeros, kv_zeros)
        state = lax.fori_loop(0, n_dev - 1, step_fn, state)
        dq_acc, k_cur, v_cur, dk_acc, dv_acc = accumulate(n_dev - 1, state)
        dk_home = lax.ppermute(dk_acc, 'cp', forward_perm)
        dv_home = lax.ppermute(dv_acc, 'cp', forward_perm)
        grad_q = (dq_acc * softmax_scale).astype(jnp.bfloat16)
        grad_k = (dk_home * softmax_scale).astype(jnp.bfloat16)
        grad_v = dv_home.astype(jnp.bfloat16)
        return grad_q, grad_k, grad_v

    return jax.shard_map(local_fn, mesh=mesh, in_specs=(row_spec, row_spec, row_spec, row_spec, row_spec, row_spec), out_specs=(row_spec, row_spec, row_spec), check_vma=False)
```

profile of v0, /device:TPU:88, one launch (start us, length us, event | category | flops | bytes accessed | tf_op | source)
XLA Modules:
  0.0 179.5 jit_solution(1274021233243226610)
XLA Ops:
  5.3 153.8 %while.21 = (s32[]{:T(128)}, f32[512,7,128]{2,0,1:T(8,128)S(1)}, bf16[512,128]{1,0:T(8,128)(2,1)S(1)}, bf16[512,128]{1,0:T(8,128)(2,1)S(1)}, f32[512,128]{1,0:T(...) while((s32[]{:T(128)}, f32[512,7,128]{2,0,1:T(8,128)S(1)}, ...), condition=%wide.region_3.4_spmd, body=%wide.region_0.3_spmd.sunk | while | flops 2368274432 | bytes 58427944 | solution.py:51
  5.4 11.6 %conditional.4 = ((f32[512,7,128]{2,0,1:T(8,128)S(1)}, f32[512,128]{1,0:T(8,128)S(1)}, f32[512,128]{1,0:T(8,128)})) conditional(s32[]{:T(128)} %convert_element_type.52, (f32[512,7,128]{2,0,1:T(8,128)S(1)}, f32[512,128]{1,0:T(8,128)S(1)}, f32[512,128]{1,0:T(8,128)}) %tuple.50, (s32[]{:T(128)}, bf16[512,7,128]{2,0,1:T(8,128)(2,1)}, ...), branch_computations={%region_1.0_spmd, %region_2.2_spmd} | conditional | flops 2368274432 | bytes 53708956 | solution.py:39
  7.9 4.0 %fusion.7 = f32[512,128]{1,0:T(8,128)} fusion(f32[512,128]{1,0:T(8,128)} %get-tuple-element.232, bf16[512,7,128]{2,0,1:T(8,128)(2,1)S(1)} %copy-done.2, f32[512,7,512]{2,0,1:T(8,128)S(1)} %fusion.14, f32[512,7]{0,1:T(8,128)S(1)} %copy-done.5, pred[512,512]{1,0:T(8,128)(4,1)S(1)} %fusion.11), kind=kOutput, calls=%fused_computation.8 | convolution fusion | flops 477167616 | bytes 9058304 | tf_op jit(solution)/shard_map/while/body/eval_jaxpr/cond/branch_1_fun/rgc,rgd->cd/dot_general | solution.py:33
  12.0 2.6 %multiply_convert_fusion = bf16[512,7,512]{2,0,1:T(8,128)(2,1)S(1)} fusion(f32[512,7,512]{2,0,1:T(8,128)S(1)} %fusion.14, f32[512,7]{0,1:T(8,128)S(1)} %get-tuple-element.230, f32[512,7]{0,1:T(8,128)S(1)} %copy-done.5, pred[512,512]{1,0:T(8,128)(4,1)S(1)} %fusion.11, bf16[512,7,128]{2,0,1:T(8,128)(2,1)S(1)} %copy-done.3, ...), kind=kOutput, calls=%fused_computation | convolution fusion | flops 480772096 | bytes 12349440 | tf_op jit(solution)/shard_map/while/body/eval_jaxpr/cond/branch_1_fun/rgd,cd->rgc/dot_general | solution.py:12
  20.5 3.5 %collective-permute-done.2 = f32[512,128]{1,0:T(8,128)S(1)} collective-permute-done((f32[512,128]{1,0:T(8,128)S(1)}, f32[512,128]{1,0:T(8,128)S(1)}, u32[]{:S(2)}, u32[]{:S(2)}) %collective-permute-start.2) | collective-permute-done | bytes 262176 | tf_op jit(solution)/shard_map/while/body/eval_jaxpr/ppermute | solution.py:45
  24.0 2.8 %collective-permute-done.3 = f32[512,128]{1,0:T(8,128)S(1)} collective-permute-done((f32[512,128]{1,0:T(8,128)}, f32[512,128]{1,0:T(8,128)S(1)}, u32[]{:S(2)}, u32[]{:S(2)}) %collective-permute-start.3) | collective-permute-done | bytes 262176 | tf_op jit(solution)/shard_map/while/body/eval_jaxpr/ppermute | solution.py:46
  29.7 9.6 %collective-permute-start.2 = (f32[512,128]{1,0:T(8,128)S(1)}, f32[512,128]{1,0:T(8,128)S(1)}, u32[]{:S(2)}, u32[]{:S(2)}) collective-permute-start(f32[512,128]{1,0:T(8,128)S(1)} %get-tuple-element.369), channel_id=1, source_target_pairs={{0,1},{1,2},{2,3},{3,4},{4,5},{5,6},{6,7},{7,0},{8,9},{9,10},{10,1... | collective-permute-start | bytes 786440 | tf_op jit(solution)/shard_map/while/body/eval_jaxpr/ppermute | solution.py:45
  44.6 2.8 %collective-permute-done.3 = f32[512,128]{1,0:T(8,128)S(1)} collective-permute-done((f32[512,128]{1,0:T(8,128)}, f32[512,128]{1,0:T(8,128)S(1)}, u32[]{:S(2)}, u32[]{:S(2)}) %collective-permute-start.3) | collective-permute-done | bytes 262176 | tf_op jit(solution)/shard_map/while/body/eval_jaxpr/ppermute | solution.py:46
  50.8 14.1 %collective-permute-start.3 = (f32[512,128]{1,0:T(8,128)}, f32[512,128]{1,0:T(8,128)S(1)}, u32[]{:S(2)}, u32[]{:S(2)}) collective-permute-start(f32[512,128]{1,0:T(8,128)} %get-tuple-element.370), channel_id=1, source_target_pairs={{0,1},{1,2},{2,3},{3,4},{4,5},{5,6},{6,7},{7,0},{8,9},{9,10},{10,1... | collective-permute-start | bytes 786440 | tf_op jit(solution)/shard_map/while/body/eval_jaxpr/ppermute | solution.py:46
  73.9 2.5 %collective-permute-start.3 = (f32[512,128]{1,0:T(8,128)}, f32[512,128]{1,0:T(8,128)S(1)}, u32[]{:S(2)}, u32[]{:S(2)}) collective-permute-start(f32[512,128]{1,0:T(8,128)} %get-tuple-element.370), channel_id=1, source_target_pairs={{0,1},{1,2},{2,3},{3,4},{4,5},{5,6},{6,7},{7,0},{8,9},{9,10},{10,1... | collective-permute-start | bytes 786440 | tf_op jit(solution)/shard_map/while/body/eval_jaxpr/ppermute | solution.py:46
  76.4 10.8 %collective-permute-start = (bf16[512,128]{1,0:T(8,128)(2,1)S(1)}, bf16[512,128]{1,0:T(8,128)(2,1)S(1)}, u32[]{:S(2)}, u32[]{:S(2)}) collective-permute-start(bf16[512,128]{1,0:T(8,128)(2,1)S(1)} %copy.36), channel_id=1, source_target_pairs={{0,1},{1,2},{2,3},{3,4},{4,5},{5,6},{6,7},{7,0},{8,9},{9,10},{10,1... | collective-permute-start | bytes 393224 | tf_op jit(solution)/shard_map/while/body/eval_jaxpr/ppermute | solution.py:43
  93.4 2.5 %collective-permute-start.3 = (f32[512,128]{1,0:T(8,128)}, f32[512,128]{1,0:T(8,128)S(1)}, u32[]{:S(2)}, u32[]{:S(2)}) collective-permute-start(f32[512,128]{1,0:T(8,128)} %get-tuple-element.370), channel_id=1, source_target_pairs={{0,1},{1,2},{2,3},{3,4},{4,5},{5,6},{6,7},{7,0},{8,9},{9,10},{10,1... | collective-permute-start | bytes 786440 | tf_op jit(solution)/shard_map/while/body/eval_jaxpr/ppermute | solution.py:46
  95.9 2.8 %collective-permute-start = (bf16[512,128]{1,0:T(8,128)(2,1)S(1)}, bf16[512,128]{1,0:T(8,128)(2,1)S(1)}, u32[]{:S(2)}, u32[]{:S(2)}) collective-permute-start(bf16[512,128]{1,0:T(8,128)(2,1)S(1)} %copy.36), channel_id=1, source_target_pairs={{0,1},{1,2},{2,3},{3,4},{4,5},{5,6},{6,7},{7,0},{8,9},{9,10},{10,1... | collective-permute-start | bytes 393224 | tf_op jit(solution)/shard_map/while/body/eval_jaxpr/ppermute | solution.py:43
  98.7 14.1 %collective-permute-start.1 = (bf16[512,128]{1,0:T(8,128)(2,1)S(1)}, bf16[512,128]{1,0:T(8,128)(2,1)S(1)}, u32[]{:S(2)}, u32[]{:S(2)}) collective-permute-start(bf16[512,128]{1,0:T(8,128)(2,1)S(1)} %copy.37), channel_id=1, source_target_pairs={{0,1},{1,2},{2,3},{3,4},{4,5},{5,6},{6,7},{7,0},{8,9},{9,10},{10,1... | collective-permute-start | bytes 393224 | tf_op jit(solution)/shard_map/while/body/eval_jaxpr/ppermute | solution.py:44
  116.2 2.5 %collective-permute-start.3 = (f32[512,128]{1,0:T(8,128)}, f32[512,128]{1,0:T(8,128)S(1)}, u32[]{:S(2)}, u32[]{:S(2)}) collective-permute-start(f32[512,128]{1,0:T(8,128)} %get-tuple-element.370), channel_id=1, source_target_pairs={{0,1},{1,2},{2,3},{3,4},{4,5},{5,6},{6,7},{7,0},{8,9},{9,10},{10,1... | collective-permute-start | bytes 786440 | tf_op jit(solution)/shard_map/while/body/eval_jaxpr/ppermute | solution.py:46
  118.7 3.1 %collective-permute-start = (bf16[512,128]{1,0:T(8,128)(2,1)S(1)}, bf16[512,128]{1,0:T(8,128)(2,1)S(1)}, u32[]{:S(2)}, u32[]{:S(2)}) collective-permute-start(bf16[512,128]{1,0:T(8,128)(2,1)S(1)} %copy.36), channel_id=1, source_target_pairs={{0,1},{1,2},{2,3},{3,4},{4,5},{5,6},{6,7},{7,0},{8,9},{9,10},{10,1... | collective-permute-start | bytes 393224 | tf_op jit(solution)/shard_map/while/body/eval_jaxpr/ppermute | solution.py:43
  121.8 2.5 %collective-permute-start.1 = (bf16[512,128]{1,0:T(8,128)(2,1)S(1)}, bf16[512,128]{1,0:T(8,128)(2,1)S(1)}, u32[]{:S(2)}, u32[]{:S(2)}) collective-permute-start(bf16[512,128]{1,0:T(8,128)(2,1)S(1)} %copy.37), channel_id=1, source_target_pairs={{0,1},{1,2},{2,3},{3,4},{4,5},{5,6},{6,7},{7,0},{8,9},{9,10},{10,1... | collective-permute-start | bytes 393224 | tf_op jit(solution)/shard_map/while/body/eval_jaxpr/ppermute | solution.py:44
  124.3 6.1 %collective-permute-done.2 = f32[512,128]{1,0:T(8,128)S(1)} collective-permute-done((f32[512,128]{1,0:T(8,128)S(1)}, f32[512,128]{1,0:T(8,128)S(1)}, u32[]{:S(2)}, u32[]{:S(2)}) %collective-permute-start.2) | collective-permute-done | bytes 262176 | tf_op jit(solution)/shard_map/while/body/eval_jaxpr/ppermute | solution.py:45
  130.5 2.8 %collective-permute-done.3 = f32[512,128]{1,0:T(8,128)S(1)} collective-permute-done((f32[512,128]{1,0:T(8,128)}, f32[512,128]{1,0:T(8,128)S(1)}, u32[]{:S(2)}, u32[]{:S(2)}) %collective-permute-start.3) | collective-permute-done | bytes 262176 | tf_op jit(solution)/shard_map/while/body/eval_jaxpr/ppermute | solution.py:46
  141.0 2.5 %collective-permute-start.1 = (bf16[512,128]{1,0:T(8,128)(2,1)S(1)}, bf16[512,128]{1,0:T(8,128)(2,1)S(1)}, u32[]{:S(2)}, u32[]{:S(2)}) collective-permute-start(bf16[512,128]{1,0:T(8,128)(2,1)S(1)} %copy.37), channel_id=1, source_target_pairs={{0,1},{1,2},{2,3},{3,4},{4,5},{5,6},{6,7},{7,0},{8,9},{9,10},{10,1... | collective-permute-start | bytes 393224 | tf_op jit(solution)/shard_map/while/body/eval_jaxpr/ppermute | solution.py:44
  143.5 10.0 %collective-permute-done.2 = f32[512,128]{1,0:T(8,128)S(1)} collective-permute-done((f32[512,128]{1,0:T(8,128)S(1)}, f32[512,128]{1,0:T(8,128)S(1)}, u32[]{:S(2)}, u32[]{:S(2)}) %collective-permute-start.2) | collective-permute-done | bytes 262176 | tf_op jit(solution)/shard_map/while/body/eval_jaxpr/ppermute | solution.py:45
  153.5 2.8 %collective-permute-done.3 = f32[512,128]{1,0:T(8,128)S(1)} collective-permute-done((f32[512,128]{1,0:T(8,128)}, f32[512,128]{1,0:T(8,128)S(1)}, u32[]{:S(2)}, u32[]{:S(2)}) %collective-permute-start.3) | collective-permute-done | bytes 262176 | tf_op jit(solution)/shard_map/while/body/eval_jaxpr/ppermute | solution.py:46
  163.5 11.8 %collective-permute-done.5 = bf16[512,128]{1,0:T(8,128)(2,1)S(1)} collective-permute-done((bf16[512,128]{1,0:T(8,128)(2,1)S(1)}, bf16[512,128]{1,0:T(8,128)(2,1)S(1)}, u32[]{:S(2)}, u32[]{:S(2)}) %collective-permute-start.5) | collective-permute-done | bytes 131104 | tf_op jit(solution)/shard_map/ppermute | solution.py:54
  175.3 2.8 %collective-permute-done.4 = f32[512,128]{1,0:T(8,128)S(1)} collective-permute-done((f32[512,128]{1,0:T(8,128)S(1)}, f32[512,128]{1,0:T(8,128)S(1)}, u32[]{:S(2)}, u32[]{:S(2)}) %collective-permute-start.4) | collective-permute-done | bytes 262176 | tf_op jit(solution)/shard_map/ppermute | solution.py:53
  (97 shorter events, 59.4 us)
Async XLA Ops:
  17.0 9.8 %collective-permute-start.3 = (f32[512,128]{1,0:T(8,128)}, f32[512,128]{1,0:T(8,128)S(1)}, u32[]{:S(2)}, u32[]{:S(2)}) collective-permute-start(f32[512,128]{1,0:T(8,128)} %get-tuple-element.370), channel_id=1, source_target_pairs={{0,1},{1,2},{2,3},{3,4},{4,5},{5,6},{6,7},{7,0},{8,9},{9,10},{10,1... | collective-permute-start | bytes 786440 | tf_op jit(solution)/shard_map/while/body/eval_jaxpr/ppermute | solution.py:46
  18.7 9.5 %collective-permute-start = (bf16[512,128]{1,0:T(8,128)(2,1)S(1)}, bf16[512,128]{1,0:T(8,128)(2,1)S(1)}, u32[]{:S(2)}, u32[]{:S(2)}) collective-permute-start(bf16[512,128]{1,0:T(8,128)(2,1)S(1)} %copy.36), channel_id=1, source_target_pairs={{0,1},{1,2},{2,3},{3,4},{4,5},{5,6},{6,7},{7,0},{8,9},{9,10},{10,1... | collective-permute-start | bytes 393224 | tf_op jit(solution)/shard_map/while/body/eval_jaxpr/ppermute | solution.py:43
  18.8 10.8 %collective-permute-start.1 = (bf16[512,128]{1,0:T(8,128)(2,1)S(1)}, bf16[512,128]{1,0:T(8,128)(2,1)S(1)}, u32[]{:S(2)}, u32[]{:S(2)}) collective-permute-start(bf16[512,128]{1,0:T(8,128)(2,1)S(1)} %copy.37), channel_id=1, source_target_pairs={{0,1},{1,2},{2,3},{3,4},{4,5},{5,6},{6,7},{7,0},{8,9},{9,10},{10,1... | collective-permute-start | bytes 393224 | tf_op jit(solution)/shard_map/while/body/eval_jaxpr/ppermute | solution.py:44
  29.7 14.9 %collective-permute-start.2 = (f32[512,128]{1,0:T(8,128)S(1)}, f32[512,128]{1,0:T(8,128)S(1)}, u32[]{:S(2)}, u32[]{:S(2)}) collective-permute-start(f32[512,128]{1,0:T(8,128)S(1)} %get-tuple-element.369), channel_id=1, source_target_pairs={{0,1},{1,2},{2,3},{3,4},{4,5},{5,6},{6,7},{7,0},{8,9},{9,10},{10,1... | collective-permute-start | bytes 786440 | tf_op jit(solution)/shard_map/while/body/eval_jaxpr/ppermute | solution.py:45
  41.9 8.3 %collective-permute-start.1 = (bf16[512,128]{1,0:T(8,128)(2,1)S(1)}, bf16[512,128]{1,0:T(8,128)(2,1)S(1)}, u32[]{:S(2)}, u32[]{:S(2)}) collective-permute-start(bf16[512,128]{1,0:T(8,128)(2,1)S(1)} %copy.37), channel_id=1, source_target_pairs={{0,1},{1,2},{2,3},{3,4},{4,5},{5,6},{6,7},{7,0},{8,9},{9,10},{10,1... | collective-permute-start | bytes 393224 | tf_op jit(solution)/shard_map/while/body/eval_jaxpr/ppermute | solution.py:44
  50.3 16.4 %collective-permute-start.2 = (f32[512,128]{1,0:T(8,128)S(1)}, f32[512,128]{1,0:T(8,128)S(1)}, u32[]{:S(2)}, u32[]{:S(2)}) collective-permute-start(f32[512,128]{1,0:T(8,128)S(1)} %get-tuple-element.369), channel_id=1, source_target_pairs={{0,1},{1,2},{2,3},{3,4},{4,5},{5,6},{6,7},{7,0},{8,9},{9,10},{10,1... | collective-permute-start | bytes 786440 | tf_op jit(solution)/shard_map/while/body/eval_jaxpr/ppermute | solution.py:45
  50.8 17.2 %collective-permute-start.3 = (f32[512,128]{1,0:T(8,128)}, f32[512,128]{1,0:T(8,128)S(1)}, u32[]{:S(2)}, u32[]{:S(2)}) collective-permute-start(f32[512,128]{1,0:T(8,128)} %get-tuple-element.370), channel_id=1, source_target_pairs={{0,1},{1,2},{2,3},{3,4},{4,5},{5,6},{6,7},{7,0},{8,9},{9,10},{10,1... | collective-permute-start | bytes 786440 | tf_op jit(solution)/shard_map/while/body/eval_jaxpr/ppermute | solution.py:46
  72.0 17.8 %collective-permute-start.2 = (f32[512,128]{1,0:T(8,128)S(1)}, f32[512,128]{1,0:T(8,128)S(1)}, u32[]{:S(2)}, u32[]{:S(2)}) collective-permute-start(f32[512,128]{1,0:T(8,128)S(1)} %get-tuple-element.369), channel_id=1, source_target_pairs={{0,1},{1,2},{2,3},{3,4},{4,5},{5,6},{6,7},{7,0},{8,9},{9,10},{10,1... | collective-permute-start | bytes 786440 | tf_op jit(solution)/shard_map/while/body/eval_jaxpr/ppermute | solution.py:45
  73.9 15.8 %collective-permute-start.3 = (f32[512,128]{1,0:T(8,128)}, f32[512,128]{1,0:T(8,128)S(1)}, u32[]{:S(2)}, u32[]{:S(2)}) collective-permute-start(f32[512,128]{1,0:T(8,128)} %get-tuple-element.370), channel_id=1, source_target_pairs={{0,1},{1,2},{2,3},{3,4},{4,5},{5,6},{6,7},{7,0},{8,9},{9,10},{10,1... | collective-permute-start | bytes 786440 | tf_op jit(solution)/shard_map/while/body/eval_jaxpr/ppermute | solution.py:46
  76.4 14.7 %collective-permute-start = (bf16[512,128]{1,0:T(8,128)(2,1)S(1)}, bf16[512,128]{1,0:T(8,128)(2,1)S(1)}, u32[]{:S(2)}, u32[]{:S(2)}) collective-permute-start(bf16[512,128]{1,0:T(8,128)(2,1)S(1)} %copy.36), channel_id=1, source_target_pairs={{0,1},{1,2},{2,3},{3,4},{4,5},{5,6},{6,7},{7,0},{8,9},{9,10},{10,1... | collective-permute-start | bytes 393224 | tf_op jit(solution)/shard_map/while/body/eval_jaxpr/ppermute | solution.py:43
  92.9 19.9 %collective-permute-start.2 = (f32[512,128]{1,0:T(8,128)S(1)}, f32[512,128]{1,0:T(8,128)S(1)}, u32[]{:S(2)}, u32[]{:S(2)}) collective-permute-start(f32[512,128]{1,0:T(8,128)S(1)} %get-tuple-element.369), channel_id=1, source_target_pairs={{0,1},{1,2},{2,3},{3,4},{4,5},{5,6},{6,7},{7,0},{8,9},{9,10},{10,1... | collective-permute-start | bytes 786440 | tf_op jit(solution)/shard_map/while/body/eval_jaxpr/ppermute | solution.py:45
  93.4 19.4 %collective-permute-start.3 = (f32[512,128]{1,0:T(8,128)}, f32[512,128]{1,0:T(8,128)S(1)}, u32[]{:S(2)}, u32[]{:S(2)}) collective-permute-start(f32[512,128]{1,0:T(8,128)} %get-tuple-element.370), channel_id=1, source_target_pairs={{0,1},{1,2},{2,3},{3,4},{4,5},{5,6},{6,7},{7,0},{8,9},{9,10},{10,1... | collective-permute-start | bytes 786440 | tf_op jit(solution)/shard_map/while/body/eval_jaxpr/ppermute | solution.py:46
  95.9 17.6 %collective-permute-start = (bf16[512,128]{1,0:T(8,128)(2,1)S(1)}, bf16[512,128]{1,0:T(8,128)(2,1)S(1)}, u32[]{:S(2)}, u32[]{:S(2)}) collective-permute-start(bf16[512,128]{1,0:T(8,128)(2,1)S(1)} %copy.36), channel_id=1, source_target_pairs={{0,1},{1,2},{2,3},{3,4},{4,5},{5,6},{6,7},{7,0},{8,9},{9,10},{10,1... | collective-permute-start | bytes 393224 | tf_op jit(solution)/shard_map/while/body/eval_jaxpr/ppermute | solution.py:43
  98.7 15.0 %collective-permute-start.1 = (bf16[512,128]{1,0:T(8,128)(2,1)S(1)}, bf16[512,128]{1,0:T(8,128)(2,1)S(1)}, u32[]{:S(2)}, u32[]{:S(2)}) collective-permute-start(bf16[512,128]{1,0:T(8,128)(2,1)S(1)} %copy.37), channel_id=1, source_target_pairs={{0,1},{1,2},{2,3},{3,4},{4,5},{5,6},{6,7},{7,0},{8,9},{9,10},{10,1... | collective-permute-start | bytes 393224 | tf_op jit(solution)/shard_map/while/body/eval_jaxpr/ppermute | solution.py:44
  113.8 16.6 %collective-permute-start.2 = (f32[512,128]{1,0:T(8,128)S(1)}, f32[512,128]{1,0:T(8,128)S(1)}, u32[]{:S(2)}, u32[]{:S(2)}) collective-permute-start(f32[512,128]{1,0:T(8,128)S(1)} %get-tuple-element.369), channel_id=1, source_target_pairs={{0,1},{1,2},{2,3},{3,4},{4,5},{5,6},{6,7},{7,0},{8,9},{9,10},{10,1... | collective-permute-start | bytes 786440 | tf_op jit(solution)/shard_map/while/body/eval_jaxpr/ppermute | solution.py:45
  116.2 17.1 %collective-permute-start.3 = (f32[512,128]{1,0:T(8,128)}, f32[512,128]{1,0:T(8,128)S(1)}, u32[]{:S(2)}, u32[]{:S(2)}) collective-permute-start(f32[512,128]{1,0:T(8,128)} %get-tuple-element.370), channel_id=1, source_target_pairs={{0,1},{1,2},{2,3},{3,4},{4,5},{5,6},{6,7},{7,0},{8,9},{9,10},{10,1... | collective-permute-start | bytes 786440 | tf_op jit(solution)/shard_map/while/body/eval_jaxpr/ppermute | solution.py:46
  118.7 16.0 %collective-permute-start = (bf16[512,128]{1,0:T(8,128)(2,1)S(1)}, bf16[512,128]{1,0:T(8,128)(2,1)S(1)}, u32[]{:S(2)}, u32[]{:S(2)}) collective-permute-start(bf16[512,128]{1,0:T(8,128)(2,1)S(1)} %copy.36), channel_id=1, source_target_pairs={{0,1},{1,2},{2,3},{3,4},{4,5},{5,6},{6,7},{7,0},{8,9},{9,10},{10,1... | collective-permute-start | bytes 393224 | tf_op jit(solution)/shard_map/while/body/eval_jaxpr/ppermute | solution.py:43
  121.8 14.3 %collective-permute-start.1 = (bf16[512,128]{1,0:T(8,128)(2,1)S(1)}, bf16[512,128]{1,0:T(8,128)(2,1)S(1)}, u32[]{:S(2)}, u32[]{:S(2)}) collective-permute-start(bf16[512,128]{1,0:T(8,128)(2,1)S(1)} %copy.37), channel_id=1, source_target_pairs={{0,1},{1,2},{2,3},{3,4},{4,5},{5,6},{6,7},{7,0},{8,9},{9,10},{10,1... | collective-permute-start | bytes 393224 | tf_op jit(solution)/shard_map/while/body/eval_jaxpr/ppermute | solution.py:44
  136.1 17.4 %collective-permute-start.2 = (f32[512,128]{1,0:T(8,128)S(1)}, f32[512,128]{1,0:T(8,128)S(1)}, u32[]{:S(2)}, u32[]{:S(2)}) collective-permute-start(f32[512,128]{1,0:T(8,128)S(1)} %get-tuple-element.369), channel_id=1, source_target_pairs={{0,1},{1,2},{2,3},{3,4},{4,5},{5,6},{6,7},{7,0},{8,9},{9,10},{10,1... | collective-permute-start | bytes 786440 | tf_op jit(solution)/shard_map/while/body/eval_jaxpr/ppermute | solution.py:45
  136.9 19.5 %collective-permute-start.3 = (f32[512,128]{1,0:T(8,128)}, f32[512,128]{1,0:T(8,128)S(1)}, u32[]{:S(2)}, u32[]{:S(2)}) collective-permute-start(f32[512,128]{1,0:T(8,128)} %get-tuple-element.370), channel_id=1, source_target_pairs={{0,1},{1,2},{2,3},{3,4},{4,5},{5,6},{6,7},{7,0},{8,9},{9,10},{10,1... | collective-permute-start | bytes 786440 | tf_op jit(solution)/shard_map/while/body/eval_jaxpr/ppermute | solution.py:46
  139.3 18.4 %collective-permute-start = (bf16[512,128]{1,0:T(8,128)(2,1)S(1)}, bf16[512,128]{1,0:T(8,128)(2,1)S(1)}, u32[]{:S(2)}, u32[]{:S(2)}) collective-permute-start(bf16[512,128]{1,0:T(8,128)(2,1)S(1)} %copy.36), channel_id=1, source_target_pairs={{0,1},{1,2},{2,3},{3,4},{4,5},{5,6},{6,7},{7,0},{8,9},{9,10},{10,1... | collective-permute-start | bytes 393224 | tf_op jit(solution)/shard_map/while/body/eval_jaxpr/ppermute | solution.py:43
  141.0 18.1 %collective-permute-start.1 = (bf16[512,128]{1,0:T(8,128)(2,1)S(1)}, bf16[512,128]{1,0:T(8,128)(2,1)S(1)}, u32[]{:S(2)}, u32[]{:S(2)}) collective-permute-start(bf16[512,128]{1,0:T(8,128)(2,1)S(1)} %copy.37), channel_id=1, source_target_pairs={{0,1},{1,2},{2,3},{3,4},{4,5},{5,6},{6,7},{7,0},{8,9},{9,10},{10,1... | collective-permute-start | bytes 393224 | tf_op jit(solution)/shard_map/while/body/eval_jaxpr/ppermute | solution.py:44
  160.1 15.2 %collective-permute-start.5 = (bf16[512,128]{1,0:T(8,128)(2,1)S(1)}, bf16[512,128]{1,0:T(8,128)(2,1)S(1)}, u32[]{:S(2)}, u32[]{:S(2)}) collective-permute-start(bf16[512,128]{1,0:T(8,128)(2,1)S(1)} %convert.12), channel_id=1, source_target_pairs={{0,1},{1,2},{2,3},{3,4},{4,5},{5,6},{6,7},{7,0},{8,9},{9,10},{10,1... | collective-permute-start | bytes 393224 | tf_op jit(solution)/shard_map/ppermute | solution.py:54
  160.2 18.0 %collective-permute-start.4 = (f32[512,128]{1,0:T(8,128)S(1)}, f32[512,128]{1,0:T(8,128)S(1)}, u32[]{:S(2)}, u32[]{:S(2)}) collective-permute-start(f32[512,128]{1,0:T(8,128)S(1)} %get-tuple-element.274), channel_id=1, source_target_pairs={{0,1},{1,2},{2,3},{3,4},{4,5},{5,6},{6,7},{7,0},{8,9},{9,10},{10,1... | collective-permute-start | bytes 786440 | tf_op jit(solution)/shard_map/ppermute | solution.py:53
  (10 other events, 52.0 us)
where the time goes:
time: 180 us; the launch traced here: 179 us
  starting transfers between devices  91.6 us (51%)
  waiting for transfers between devices  62.1 us (34%)
  matrix products  11.4 us (6%)
  local copies, waits for them, and re-layouts  8.54 us (5%)
  other arithmetic  4.86 us (3%)
    ppermute x7, starting transfers between devices, step_fn(): dv_next = lax.ppermute(dv_acc, 'cp', forward_perm)  28.2 us
    ppermute x7, starting transfers between devices, step_fn(): v_next = lax.ppermute(v_cur, 'cp', forward_perm)  26.6 us
    ppermute x7, waiting for transfers between devices, step_fn(): dk_next = lax.ppermute(dk_acc, 'cp', forward_perm)  20.7 us
    ppermute x7, starting transfers between devices, step_fn(): k_next = lax.ppermute(k_cur, 'cp', forward_perm)  18.6 us
    ppermute x7, starting transfers between devices, step_fn(): dk_next = lax.ppermute(dk_acc, 'cp', forward_perm)  15.9 us
    ppermute x7, waiting for transfers between devices, step_fn(): dv_next = lax.ppermute(dv_acc, 'cp', forward_perm)  12.5 us
    ppermute x1, waiting for transfers between devices, local_fn(): dv_home = lax.ppermute(dv_acc, 'cp', forward_perm)  11.8 us
    ppermute x7, waiting for transfers between devices, step_fn(): v_next = lax.ppermute(v_cur, 'cp', forward_perm)  8.99 us
  transfers between devices with their start and end apart: 30, of which 24 were waited for; matrix products, arithmetic and copies ran while one was open for 3% of the time, Pallas kernels for 0%

commit v1 on v0

v1 whole, which is shorter than its diff:
```python
import functools

import jax
import jax.numpy as jnp
from jax import lax
from jax.experimental import pallas as pl
from jax.experimental.pallas import tpu as pltpu
from jax.sharding import PartitionSpec as P

LOG2E = 1.4426950408889634
MESH = pl.DeviceIdType.MESH
NT = ((1,), (1,))
NN = ((1,), (0,))


def dot(lhs, rhs, dims):
    return lax.dot_general(lhs, rhs, (dims, ((), ())), preferred_element_type=jnp.float32)


def wide(column, width):
    return jnp.concatenate([column] * (width // column.shape[1]), axis=1)


def attention_kernel(n_dev, softmax_scale, q_hbm, k_hbm, v_hbm, o_hbm, do_hbm, lse_hbm, dq_hbm, dk_hbm, dv_hbm,
                     q_ref, do_ref, o_ref, lse_ref, kv_ref, q_t, do_t, lse_col, delta_col, dq_acc, acc, p_buf, s_buf,
                     from_core, from_chip, dq_out, dkv_out,
                     load_sem, store_sem, kv_send, kv_recv, core_send, core_recv, chip_send, chip_recv):
    heads, rows, dim = q_ref.shape
    half = rows // 2
    n_chips = n_dev // 2
    me = lax.axis_index('cp')
    chip, core = me // 2, lax.rem(me, 2)
    partner = 2 * chip + 1 - core
    log_scale = softmax_scale * LOG2E

    barrier = pltpu.get_barrier_semaphore()
    for step in range(1, n_dev):
        pl.semaphore_signal(barrier, inc=1, device_id={'cp': lax.rem(me + step, n_dev)}, device_id_type=MESH)

    loads = [
        pltpu.make_async_copy(k_hbm, kv_ref.at[me, 0], load_sem.at[0]),
        pltpu.make_async_copy(v_hbm, kv_ref.at[me, 1], load_sem.at[1]),
        pltpu.make_async_copy(q_hbm, q_ref, load_sem.at[2]),
        pltpu.make_async_copy(do_hbm, do_ref, load_sem.at[3]),
        pltpu.make_async_copy(lse_hbm, lse_ref, load_sem.at[4]),
        pltpu.make_async_copy(o_hbm, o_ref, load_sem.at[5]),
    ]
    for load in loads:
        load.start()

    def remote(src, dst, send, recv, target):
        return pltpu.make_async_remote_copy(src_ref=src, dst_ref=dst, send_sem=send, recv_sem=recv, device_id={'cp': target}, device_id_type=MESH)

    def kv_to_chip(far):
        return remote(kv_ref.at[me], kv_ref.at[me], kv_send.at[far], kv_recv.at[me], me + 2 * far)

    def kv_to_partner():
        return remote(kv_ref.at[me], kv_ref.at[me], kv_send.at[0], kv_recv.at[me], partner)

    def kv_forward(stage):
        block = 2 * (chip - 1 - stage) + core
        return remote(kv_ref.at[block], kv_ref.at[block], kv_send.at[n_chips + stage], kv_recv.at[block], partner)

    def wait_kv(block):
        remote(kv_ref.at[block], kv_ref.at[block], kv_send.at[0], kv_recv.at[block], partner).wait_recv()

    def sum_to_partner(block, slot):
        return remote(acc.at[block], from_core.at[slot], core_send.at[slot], core_recv.at[slot], partner)

    def sum_to_owner(stage):
        block = 2 * (chip - 1 - stage) + core
        return remote(acc.at[block], from_chip.at[stage], chip_send.at[stage], chip_recv.at[stage], block)

    loads[0].wait()
    loads[1].wait()
    pl.semaphore_wait(barrier, n_dev - 1)
    for far in range(1, n_chips):
        @pl.when(chip + far < n_chips)
        def _():
            kv_to_chip(far).start()

    @pl.when(core == 0)
    def _():
        kv_to_partner().start()

    for load in loads[2:]:
        load.wait()

    def prepare(head):
        q_t[head] = q_ref[head].T
        do_t[head] = do_ref[head].T
        lse_col[head] = jnp.broadcast_to(lse_ref[pl.ds(head, 1), :] * LOG2E, (dim, rows)).T
        delta = jnp.sum(do_ref[head].astype(jnp.float32) * o_ref[head].astype(jnp.float32), axis=1, keepdims=True)
        delta_col[head] = jnp.broadcast_to(delta, (rows, dim))

    def tile(block, head, slot, row_at, col_at, diagonal):
        on_rows, on_cols = slice(row_at, rows), slice(col_at, col_at + half)
        prob = jnp.exp2(dot(q_ref[head, on_rows], kv_ref[block, 0, on_cols], NT) * log_scale - wide(lse_col[head, on_rows], half))
        if diagonal:
            row_ids = lax.broadcasted_iota(jnp.int32, prob.shape, 0)
            col_ids = lax.broadcasted_iota(jnp.int32, prob.shape, 1)
            prob = jnp.where(col_ids <= row_ids, prob, 0.0)
        d_prob = dot(do_ref[head, on_rows], kv_ref[block, 1, on_cols], NT)
        score = prob * (d_prob - wide(delta_col[head, on_rows], half))
        p_buf[slot, on_rows, on_cols] = prob.astype(jnp.bfloat16)
        s_buf[slot, on_rows, on_cols] = score.astype(jnp.bfloat16)

    def add_to(ref, index, value, first):
        if first:
            ref[index] = value
        else:
            ref[index] += value

    def own_block(block):
        for step in range(heads + 1):
            if step < heads:
                tile(block, step, step % 2, 0, 0, True)
                tile(block, step, step % 2, half, half, True)
            if step >= 1:
                head, slot = step - 1, (step - 1) % 2
                first = head == 0
                left, right, low = slice(0, half), slice(half, rows), slice(half, rows)
                add_to(acc, (block, 1, slice(None), left), dot(do_t[head], p_buf[slot, :, left], NN), first)
                add_to(acc, (block, 0, slice(None), left), dot(q_t[head], s_buf[slot, :, left], NN), first)
                add_to(acc, (block, 1, slice(None), right), dot(do_t[head, :, low], p_buf[slot, low, right], NN), first)
                add_to(acc, (block, 0, slice(None), right), dot(q_t[head, :, low], s_buf[slot, low, right], NN), first)
                dq_acc[head, left] = dot(s_buf[slot, left, left], kv_ref[block, 0, left], NN)
                dq_acc[head, low] = dot(s_buf[slot, low, :], kv_ref[block, 0], NN)

    def full_block(block):
        for step in range(heads + 1):
            if step < heads:
                tile(block, step, step % 2, 0, 0, False)
                tile(block, step, step % 2, 0, half, False)
            if step >= 1:
                head, slot = step - 1, (step - 1) % 2
                prob, score = p_buf[slot], s_buf[slot]
                add_to(acc, (block, 1), dot(do_t[head], prob, NN), head == 0)
                add_to(acc, (block, 0), dot(q_t[head], score, NN), head == 0)
                dq_acc[head] += dot(score, kv_ref[block, 0], NN)

    def prepare_one(head, _):
        prepare(head)
        return 0

    lax.fori_loop(0, heads, prepare_one, 0)
    own_block(me)

    def merge(stage):
        block = 2 * (chip - 1 - stage) + core
        sum_to_partner(block, stage).wait_recv()
        acc[block] += from_core[stage]
        sum_to_owner(stage).start()

    def visit(turn, _):
        stage, second = turn // 2, lax.rem(turn, 2)
        is_local = turn == 2 * chip
        mine = jnp.logical_and(jnp.logical_not(is_local), (turn == 0) | ((second == 1) & (stage >= 1)))
        parity = jnp.where(mine, core, 1 - core)
        block = jnp.where(is_local, 2 * chip, 2 * (chip - 1 - stage) + parity)

        ahead = (turn + 1) // 2

        @pl.when(((turn == 0) | (second == 1)) & (ahead < chip))
        def _():
            wait_kv(2 * (chip - 1 - ahead) + core)
            kv_forward(ahead).start()

        @pl.when(jnp.logical_not(mine))
        def _():
            wait_kv(block)

        full_block(block)

        @pl.when(jnp.logical_not(mine))
        def _():
            sum_to_partner(block, jnp.where(is_local, n_chips - 1, stage)).start()

        @pl.when((turn == 2) & (chip >= 2))
        def _():
            merge(0)

        @pl.when((turn == 1) & (chip == 1))
        def _():
            merge(0)

        @pl.when((second == 1) & (stage >= 1))
        def _():
            merge(stage)

        return 0

    lax.fori_loop(0, me, visit, 0)

    for head in range(heads):
        dq_out[head] = (dq_acc[head] * softmax_scale).astype(jnp.bfloat16)
    store_dq = pltpu.make_async_copy(dq_out, dq_hbm, store_sem.at[0])
    store_dq.start()

    @pl.when(core == 0)
    def _():
        sum_to_partner(me, n_chips - 1).wait_recv()
        acc[me] += from_core[n_chips - 1]

    for far in range(1, n_chips):
        @pl.when(chip + far < n_chips)
        def _():
            remote(acc.at[me], from_chip.at[far - 1], chip_send.at[far - 1], chip_recv.at[far - 1], partner).wait_recv()
            acc[me] += from_chip[far - 1]

    dkv_out[0] = (acc[me, 0] * softmax_scale).T.astype(jnp.bfloat16)
    store_dk = pltpu.make_async_copy(dkv_out.at[0], dk_hbm, store_sem.at[1])
    store_dk.start()
    dkv_out[1] = acc[me, 1].T.astype(jnp.bfloat16)
    store_dv = pltpu.make_async_copy(dkv_out.at[1], dv_hbm, store_sem.at[2])
    store_dv.start()

    for far in range(1, n_chips):
        @pl.when(chip + far < n_chips)
        def _():
            kv_to_chip(far).wait_send()

    @pl.when(core == 0)
    def _():
        kv_to_partner().wait_send()

    @pl.when(core == 1)
    def _():
        sum_to_partner(2 * chip, n_chips - 1).wait_send()

    def finish(stage, _):
        kv_forward(stage).wait_send()
        sum_to_partner(2 * (chip - 1 - stage) + 1 - core, stage).wait_send()
        sum_to_owner(stage).wait_send()
        return 0

    lax.fori_loop(0, chip, finish, 0)
    store_dq.wait()
    store_dk.wait()
    store_dv.wait()


def solution(mesh):
    n_dev = mesh.shape['cp']
    n_chips = n_dev // 2
    row_spec = P(('dp', 'cp'))
    f32, bf16 = jnp.float32, jnp.bfloat16

    def local_fn(q_tok, k_tok, v_tok, fwd_out, d_out, lse_row):
        rows, heads, dim = q_tok.shape
        per_head = (heads, rows, dim)
        in_hbm = pl.BlockSpec(memory_space=pl.ANY)
        dma = pltpu.SemaphoreType.DMA
        grad_q, grad_k, grad_v = pl.pallas_call(
            functools.partial(attention_kernel, n_dev, dim ** -0.5),
            out_shape=(
                jax.ShapeDtypeStruct(per_head, bf16),
                jax.ShapeDtypeStruct((rows, dim), bf16),
                jax.ShapeDtypeStruct((rows, dim), bf16),
            ),
            in_specs=[in_hbm] * 6,
            out_specs=(in_hbm, in_hbm, in_hbm),
            scratch_shapes=[
                pltpu.VMEM(per_head, bf16),
                pltpu.VMEM(per_head, bf16),
                pltpu.VMEM(per_head, bf16),
                pltpu.VMEM((heads, rows), f32),
                pltpu.VMEM((n_dev, 2, rows, dim), bf16),
                pltpu.VMEM((heads, dim, rows), bf16),
                pltpu.VMEM((heads, dim, rows), bf16),
                pltpu.VMEM(per_head, f32),
                pltpu.VMEM(per_head, f32),
                pltpu.VMEM(per_head, f32),
                pltpu.VMEM((n_dev, 2, dim, rows), f32),
                pltpu.VMEM((2, rows, rows), bf16),
                pltpu.VMEM((2, rows, rows), bf16),
                pltpu.VMEM((n_chips, 2, dim, rows), f32),
                pltpu.VMEM((n_chips - 1, 2, dim, rows), f32),
                pltpu.VMEM(per_head, bf16),
                pltpu.VMEM((2, rows, dim), bf16),
                dma((6,)),
                dma((3,)),
                dma((2 * n_chips,)),
                dma((n_dev,)),
                dma((n_chips,)),
                dma((n_chips,)),
                dma((n_chips - 1,)),
                dma((n_chips - 1,)),
            ],
            compiler_params=pltpu.CompilerParams(collective_id=0, has_side_effects=True),
            name='attention_grad',
        )(q_tok.transpose(1, 0, 2), k_tok, v_tok, fwd_out.transpose(1, 0, 2), d_out.transpose(1, 0, 2), lse_row.T)
        return grad_q.transpose(1, 0, 2), grad_k, grad_v

    return jax.shard_map(local_fn, mesh=mesh, in_specs=(row_spec,) * 6, out_specs=(row_spec,) * 3, check_vma=False)
```

time: 180 us -> 61.1 us (0.34)
  the two profiles are of different devices: /device:TPU:88 before, /device:TPU:81 now
where the time goes in v1:
time: 61.1 us; the launch traced here: 61 us
  Pallas kernels  56.5 us (92%)
  local copies, waits for them, and re-layouts  3.81 us (6%)
  between operations  0.65 us (1%)
    pallas_call x1, Pallas kernels, local_fn(): pl.pallas_call(functools.partial(attention_kernel, n_dev, dim ** (-0.5)),...  56.5 us
    unnamed x7, local copies, waits for them, and re-layouts  3.81 us

profile of v1, /device:TPU:81, one launch (start us, length us, event | category | flops | bytes accessed | tf_op | source)
XLA Modules:
  0.0 61.0 jit_solution(3121705489850086431)
XLA Ops:
  0.6 56.5 %attention_grad.1 = (bf16[7,512,128]{2,1,0:T(8,128)(2,1)}, bf16[512,128]{1,0:T(8,128)(2,1)}, bf16[512,128]{1,0:T(8,128)(2,1)}) custom-call(bf16[7,512,128]{2,1,0:T(8,128)(2,1)} %bitcast.6, bf16[512,128]{1,0:T(8,128)(2,1)} %k_hbm.1, bf16[512,128]{1,0:T(8,128)(2,1)} %v_hbm.1, bf16[7,512,128]{2,1,0:T(8,128)(2,1)} %bitcast.7, bf16[7,512,128]{2,1,0:T(8,128)(2,1)} %bitcast.8, ...), custom_call_target="tpu_custom_call" | custom-call | tf_op jit(solution)/shard_map/attention_grad/pallas_call | solution.py:254
  57.2 0.0 copy-start.1
  57.2 2.2 %copy.12 = bf16[512,7,128]{2,0,1:T(8,128)(2,1)} copy(bf16[512,7,128]{2,0,1:T(8,128)(2,1)} %bitcast.5) | data formatting | bytes 1835008
  59.4 0.0 copy-done.1
  59.4 0.0 copy-start
  59.4 0.7 %copy.13 = bf16[512,128]{1,0:T(8,128)(2,1)} copy(bf16[512,128]{1,0:T(8,128)(2,1)S(1)} %copy-done.1) | data formatting | bytes 262144
  60.0 0.3 copy-done
  60.3 0.7 %copy.14 = bf16[512,128]{1,0:T(8,128)(2,1)} copy(bf16[512,128]{1,0:T(8,128)(2,1)S(1)} %copy-done) | data formatting | bytes 262144
Async XLA Ops:
  57.2 2.2 %copy-start.1 = (bf16[512,128]{1,0:T(8,128)(2,1)S(1)}, bf16[512,128]{1,0:T(8,128)(2,1)}, u32[]{:S(2)}) copy-start(bf16[512,128]{1,0:T(8,128)(2,1)} %get-tuple-element.13) | copy-start | bytes 393220
  59.4 1.0 %copy-start = (bf16[512,128]{1,0:T(8,128)(2,1)S(1)}, bf16[512,128]{1,0:T(8,128)(2,1)}, u32[]{:S(2)}) copy-start(bf16[512,128]{1,0:T(8,128)(2,1)} %get-tuple-element.14) | copy-start | bytes 393220

commit v2 on v0

v2 whole, which is shorter than its diff:
```python
import functools

import jax
import jax.numpy as jnp
from jax import lax
from jax.experimental import pallas as pl
from jax.experimental.pallas import tpu as pltpu
from jax.sharding import PartitionSpec as P

LOG2E = 1.4426950408889634
MESH = pl.DeviceIdType.MESH
NT = ((1,), (1,))
NN = ((1,), (0,))


def dot(lhs, rhs, dims):
    return lax.dot_general(lhs, rhs, (dims, ((), ())), preferred_element_type=jnp.float32)


def wide(column, width):
    return jnp.concatenate([column] * (width // column.shape[1]), axis=1)


def attention_kernel(n_dev, softmax_scale, q_hbm, k_hbm, v_hbm, o_hbm, do_hbm, lse_hbm, dq_ref, dk_ref, dv_ref,
                     q_ref, do_ref, o_ref, lse_ref, kv_ref, q_t, do_t, lse_col, delta_col, dq_acc, acc, p_buf, s_buf,
                     from_core, from_chip,
                     load_sem, own_send, forward_send, kv_recv, core_send, core_recv, chip_send, chip_recv):
    heads, rows, dim = q_ref.shape
    half = rows // 2
    n_chips = n_dev // 2
    local = n_chips - 1
    me = lax.axis_index('cp')
    chip, core = me // 2, lax.rem(me, 2)
    partner = 2 * chip + 1 - core
    log_scale = softmax_scale * LOG2E

    barrier = pltpu.get_barrier_semaphore()
    for step in range(1, n_dev):
        pl.semaphore_signal(barrier, inc=1, device_id={'cp': lax.rem(me + step, n_dev)}, device_id_type=MESH)

    kv_loads = []
    for part in range(2):
        on_part = pl.ds(part * half, half)
        kv_loads.append(pltpu.make_async_copy(k_hbm.at[on_part], kv_ref.at[me, part, 0], load_sem.at[2 * part]))
        kv_loads.append(pltpu.make_async_copy(v_hbm.at[on_part], kv_ref.at[me, part, 1], load_sem.at[2 * part + 1]))
    loads = [
        pltpu.make_async_copy(q_hbm, q_ref, load_sem.at[4]),
        pltpu.make_async_copy(do_hbm, do_ref, load_sem.at[5]),
        pltpu.make_async_copy(lse_hbm, lse_ref, load_sem.at[6]),
        pltpu.make_async_copy(o_hbm, o_ref, load_sem.at[7]),
    ]
    for load in kv_loads + loads:
        load.start()

    def remote(src, dst, send, recv, target):
        return pltpu.make_async_remote_copy(src_ref=src, dst_ref=dst, send_sem=send, recv_sem=recv, device_id={'cp': target}, device_id_type=MESH)

    def owner_chip(stage):
        return jnp.where((chip == n_chips - 1) & (stage < 2), 1 - stage, stage)

    def kv_to_chip(far, part):
        return remote(kv_ref.at[me, part], kv_ref.at[me, part], own_send.at[far, part], kv_recv.at[me, part], me + 2 * far)

    def kv_to_partner(part):
        return remote(kv_ref.at[me, part], kv_ref.at[me, part], own_send.at[0, part], kv_recv.at[me, part], partner)

    def kv_forward(stage, part):
        block = 2 * owner_chip(stage) + core
        return remote(kv_ref.at[block, part], kv_ref.at[block, part], forward_send.at[stage, part], kv_recv.at[block, part], partner)

    def wait_kv(block, part):
        remote(kv_ref.at[block, part], kv_ref.at[block, part], own_send.at[0, part], kv_recv.at[block, part], partner).wait_recv()

    def receive(stage, part):
        wait_kv(2 * owner_chip(stage) + core, part)
        kv_forward(stage, part).start()

    def sum_to_partner(block, slot, part):
        return remote(acc.at[block, part], from_core.at[slot, part], core_send.at[slot, part], core_recv.at[slot, part], partner)

    def sum_to_owner(stage, part):
        owner = owner_chip(stage)
        block, slot = 2 * owner + core, chip - owner - 1
        return remote(acc.at[block, part], from_chip.at[slot, part], chip_send.at[stage, part], chip_recv.at[slot, part], block)

    def merge(stage, part):
        block = 2 * owner_chip(stage) + core
        sum_to_partner(block, stage, part).wait_recv()
        acc[block, part] += from_core[stage, part]
        sum_to_owner(stage, part).start()

    def on_later_chips(action, fars):
        for far in fars:
            @pl.when(chip + far < n_chips)
            def _():
                for part in range(2):
                    action(far, part)

    for load in kv_loads:
        load.wait()
    pl.semaphore_wait(barrier, n_dev - 1)
    on_later_chips(lambda far, part: kv_to_chip(far, part).start(), range(n_chips - 2, 0, -1))

    @pl.when(core == 0)
    def _():
        for part in range(2):
            kv_to_partner(part).start()

    for load in loads:
        load.wait()

    def prepare(head, _):
        q_t[head] = q_ref[head].T
        do_t[head] = do_ref[head].T
        lse_col[head] = jnp.broadcast_to(lse_ref[pl.ds(head, 1), :] * LOG2E, (dim, rows)).T
        delta = jnp.sum(do_ref[head].astype(jnp.float32) * o_ref[head].astype(jnp.float32), axis=1, keepdims=True)
        delta_col[head] = jnp.broadcast_to(delta, (rows, dim))
        return 0

    lax.fori_loop(0, heads, prepare, 0)

    def tile(block, part, head, slot, row_at, col_at, diagonal):
        on_rows, on_cols = slice(row_at, rows), slice(col_at, col_at + half)
        prob = jnp.exp2(dot(q_ref[head, on_rows], kv_ref[block, part, 0], NT) * log_scale - wide(lse_col[head, on_rows], half))
        if diagonal:
            row_ids = lax.broadcasted_iota(jnp.int32, prob.shape, 0)
            col_ids = lax.broadcasted_iota(jnp.int32, prob.shape, 1)
            prob = jnp.where(col_ids <= row_ids, prob, 0.0)
        d_prob = dot(do_ref[head, on_rows], kv_ref[block, part, 1], NT)
        score = prob * (d_prob - wide(delta_col[head, on_rows], half))
        p_buf[slot, on_rows, on_cols] = prob.astype(jnp.bfloat16)
        s_buf[slot, on_rows, on_cols] = score.astype(jnp.bfloat16)

    def add_to(ref, index, value, first):
        if first:
            ref[index] = value
        else:
            ref[index] += value

    def add_sums(block, part, head, slot, row_at, col_at):
        on_rows, on_cols = slice(row_at, rows), slice(col_at, col_at + half)
        add_to(acc, (block, part, 1), dot(do_t[head, :, on_rows], p_buf[slot, on_rows, on_cols], NN), head == 0)
        add_to(acc, (block, part, 0), dot(q_t[head, :, on_rows], s_buf[slot, on_rows, on_cols], NN), head == 0)

    def keys(block):
        return jnp.concatenate([kv_ref[block, 0, 0], kv_ref[block, 1, 0]], axis=0)

    def staggered(make, use):
        for step in range(heads + 1):
            if step < heads:
                make(step, step % 2)
            if step >= 1:
                use(step - 1, (step - 1) % 2)

    def own_block(block):
        def make(head, slot):
            tile(block, 0, head, slot, 0, 0, True)
            tile(block, 1, head, slot, half, half, True)

        def use(head, slot):
            add_sums(block, 0, head, slot, 0, 0)
            add_sums(block, 1, head, slot, half, half)
            dq_acc[head, 0:half] = dot(s_buf[slot, 0:half, 0:half], kv_ref[block, 0, 0], NN)
            dq_acc[head, half:rows] = dot(s_buf[slot, half:rows, :], keys(block), NN)

        staggered(make, use)

    def full_block(block):
        def make(head, slot):
            tile(block, 0, head, slot, 0, 0, False)
            tile(block, 1, head, slot, 0, half, False)

        def use(head, slot):
            add_sums(block, 0, head, slot, 0, 0)
            add_sums(block, 1, head, slot, 0, half)
            dq_acc[head] += dot(s_buf[slot], keys(block), NN)

        staggered(make, use)

    def half_block(block, part):
        def make(head, slot):
            tile(block, part, head, slot, 0, 0, False)

        def use(head, slot):
            add_sums(block, part, head, slot, 0, 0)
            dq_acc[head] += dot(s_buf[slot, :, 0:half], kv_ref[block, part, 0], NN)

        staggered(make, use)

    own_block(me)
    on_later_chips(lambda far, part: kv_to_chip(far, part).start(), [n_chips - 1])

    def visit(turn, _):
        stage, quarter = turn // 4, lax.rem(turn, 4)
        part, odd = quarter // 2, lax.rem(quarter, 2)
        mine = jnp.where(stage == 0, 1 - odd, odd)
        block = 2 * owner_chip(stage) + jnp.where(mine == 1, core, 1 - core)

        @pl.when((stage == 0) & (odd == 0))
        def _():
            receive(0, part)

        @pl.when((quarter == 3) & (stage + 1 < chip))
        def _():
            receive(stage + 1, 0)

        @pl.when((quarter == 1) & (stage >= 1))
        def _():
            receive(stage, 1)

        @pl.when(mine == 0)
        def _():
            wait_kv(block, part)

        half_block(block, part)

        @pl.when(mine == 0)
        def _():
            sum_to_partner(block, stage, part).start()

        @pl.when((stage == 0) & (quarter == 2))
        def _():
            merge(0, 0)

        @pl.when(((stage == 0) & (quarter == 3) & (chip == 1)) | ((stage == 1) & (quarter == 0)))
        def _():
            merge(0, 1)

        @pl.when((stage >= 1) & (odd == 1))
        def _():
            merge(stage, part)

        return 0

    lax.fori_loop(0, 4 * chip, visit, 0)

    @pl.when(core == 1)
    def _():
        for part in range(2):
            wait_kv(2 * chip, part)
        full_block(2 * chip)
        for part in range(2):
            sum_to_partner(2 * chip, local, part).start()

    for head in range(heads):
        dq_ref[head] = (dq_acc[head] * softmax_scale).astype(jnp.bfloat16)

    @pl.when(core == 0)
    def _():
        for part in range(2):
            sum_to_partner(me, local, part).wait_recv()
        acc[me] += from_core[local]

    def collect(far, part):
        remote(acc.at[me, part], from_chip.at[far - 1, part], chip_send.at[far - 1, part], chip_recv.at[far - 1, part], partner).wait_recv()
        acc[me, part] += from_chip[far - 1, part]

    on_later_chips(collect, range(1, n_chips))
    for part in range(2):
        on_part = slice(part * half, (part + 1) * half)
        dk_ref[on_part] = (acc[me, part, 0] * softmax_scale).T.astype(jnp.bfloat16)
        dv_ref[on_part] = acc[me, part, 1].T.astype(jnp.bfloat16)

    on_later_chips(lambda far, part: kv_to_chip(far, part).wait_send(), range(1, n_chips))

    @pl.when(core == 0)
    def _():
        for part in range(2):
            kv_to_partner(part).wait_send()

    @pl.when(core == 1)
    def _():
        for part in range(2):
            sum_to_partner(2 * chip, local, part).wait_send()

    def finish(stage, _):
        for part in range(2):
            kv_forward(stage, part).wait_send()
            sum_to_partner(2 * owner_chip(stage) + 1 - core, stage, part).wait_send()
            sum_to_owner(stage, part).wait_send()
        return 0

    lax.fori_loop(0, chip, finish, 0)


def store_kernel(dq_ref, dk_ref, dv_ref, dq_hbm, dk_hbm, dv_hbm, sem):
    stores = [
        pltpu.make_async_copy(dq_ref, dq_hbm, sem.at[0]),
        pltpu.make_async_copy(dk_ref, dk_hbm, sem.at[1]),
        pltpu.make_async_copy(dv_ref, dv_hbm, sem.at[2]),
    ]
    for store in stores:
        store.start()
    for store in stores:
        store.wait()


def solution(mesh):
    n_dev = mesh.shape['cp']
    n_chips = n_dev // 2
    row_spec = P(('dp', 'cp'))
    f32, bf16 = jnp.float32, jnp.bfloat16

    def local_fn(q_tok, k_tok, v_tok, fwd_out, d_out, lse_row):
        rows, heads, dim = q_tok.shape
        half = rows // 2
        per_head = (heads, rows, dim)
        anywhere = pl.BlockSpec(memory_space=pl.ANY)
        in_vmem = pl.BlockSpec(memory_space=pltpu.VMEM)
        dma = pltpu.SemaphoreType.DMA
        operands = (q_tok.transpose(1, 0, 2), k_tok, v_tok, fwd_out.transpose(1, 0, 2), d_out.transpose(1, 0, 2), lse_row.T)
        grads = pl.pallas_call(
            functools.partial(attention_kernel, n_dev, dim ** -0.5),
            out_shape=(pltpu.VMEM(per_head, bf16), pltpu.VMEM((rows, dim), bf16), pltpu.VMEM((rows, dim), bf16)),
            in_specs=[anywhere] * 6,
            out_specs=(in_vmem, in_vmem, in_vmem),
            scratch_shapes=[
                pltpu.VMEM(per_head, bf16),
                pltpu.VMEM(per_head, bf16),
                pltpu.VMEM(per_head, bf16),
                pltpu.VMEM((heads, rows), f32),
                pltpu.VMEM((n_dev, 2, 2, half, dim), bf16),
                pltpu.VMEM((heads, dim, rows), bf16),
                pltpu.VMEM((heads, dim, rows), bf16),
                pltpu.VMEM(per_head, f32),
                pltpu.VMEM(per_head, f32),
                pltpu.VMEM(per_head, f32),
                pltpu.VMEM((n_dev, 2, 2, dim, half), f32),
                pltpu.VMEM((2, rows, rows), bf16),
                pltpu.VMEM((2, rows, rows), bf16),
                pltpu.VMEM((n_chips, 2, 2, dim, half), f32),
                pltpu.VMEM((n_chips - 1, 2, 2, dim, half), f32),
                dma((8,)),
                dma((n_chips, 2)),
                dma((n_chips - 1, 2)),
                dma((n_dev, 2)),
                dma((n_chips, 2)),
                dma((n_chips, 2)),
                dma((n_chips - 1, 2)),
                dma((n_chips - 1, 2)),
            ],
            compiler_params=pltpu.CompilerParams(collective_id=0, has_side_effects=True, vmem_limit_bytes=40 * 2**20),
            name='attention_grad',
        )(*[pltpu.with_memory_space_constraint(operand, pltpu.HBM) for operand in operands])
        grad_q, grad_k, grad_v = pl.pallas_call(
            store_kernel,
            out_shape=[jax.ShapeDtypeStruct(grad.shape, bf16) for grad in grads],
            in_specs=[in_vmem] * 3,
            out_specs=[anywhere] * 3,
            scratch_shapes=[dma((3,))],
            compiler_params=pltpu.CompilerParams(vmem_limit_bytes=2**20),
            name='store_grads',
        )(*grads)
        return grad_q.transpose(1, 0, 2), grad_k, grad_v

    return jax.shard_map(local_fn, mesh=mesh, in_specs=(row_spec,) * 6, out_specs=(row_spec,) * 3, check_vma=False)
```

time: 180 us -> 45.5 us (0.25)
  the two profiles are of different devices: /device:TPU:88 before, /device:TPU:84 now
where the time goes in v2:
time: 45.5 us; the launch traced here: 45.3 us
  Pallas kernels  44.7 us (98%)
  between operations  0.64 us (1%)
    pallas_call x1, Pallas kernels, local_fn(): pl.pallas_call(functools.partial(attention_kernel, n_dev, dim ** (-0.5)),...  43.7 us
    pallas_call x1, Pallas kernels, local_fn(): pl.pallas_call(store_kernel, out_shape=[jax.ShapeDtypeStruct(grad.shape,...  1.03 us

profile of v2, /device:TPU:84, one launch (start us, length us, event | category | flops | bytes accessed | tf_op | source)
XLA Modules:
  0.0 45.3 jit_solution(12121766349188273947)
XLA Ops:
  0.6 43.7 %attention_grad.1 = (bf16[7,512,128]{2,1,0:T(8,128)(2,1)S(1)}, bf16[512,128]{1,0:T(8,128)(2,1)S(1)}, bf16[512,128]{1,0:T(8,128)(2,1)S(1)}) custom-call(bf16[7,512,128]{2,1,0:T(8,128)(2,1)} %bitcast.5, bf16[512,128]{1,0:T(8,128)(2,1)} %k_hbm.1, bf16[512,128]{1,0:T(8,128)(2,1)} %v_hbm.1, bf16[7,512,128]{2,1,0:T(8,128)(2,1)} %bitcast.6, ...), custom_call_target="tpu_custom_call" | custom-call | tf_op jit(solution)/shard_map/attention_grad/pallas_call | solution.py:312
  44.3 1.0 %store_grads.1 = (bf16[7,512,128]{2,1,0:T(8,128)(2,1)}, bf16[512,128]{1,0:T(8,128)(2,1)}, bf16[512,128]{1,0:T(8,128)(2,1)}) custom-call(bf16[7,512,128]{2,1,0:T(8,128)(2,1)S(1)} %get-tuple-element.9.dq_ref, bf16[512,128]{1,0:T(8,128)(2,1)S(1)} %get-tuple-element.10.dk_ref, bf16[512,128]{1,0:T(8,128)(2,1)S(1)} %get-tuple-element.11.dv_ref), custom_call_target="tpu_custom_call" | custom-call | tf_op jit(solution)/shard_map/store_grads/pallas_call | solution.py:345

commit v3 on v2

--- a/solution.py
+++ b/solution.py
@@ -43,20 +43,28 @@
         on_part = pl.ds(part * half, half)
         kv_loads.append(pltpu.make_async_copy(k_hbm.at[on_part], kv_ref.at[me, part, 0], load_sem.at[2 * part]))
         kv_loads.append(pltpu.make_async_copy(v_hbm.at[on_part], kv_ref.at[me, part, 1], load_sem.at[2 * part + 1]))
-    loads = [
-        pltpu.make_async_copy(q_hbm, q_ref, load_sem.at[4]),
-        pltpu.make_async_copy(do_hbm, do_ref, load_sem.at[5]),
-        pltpu.make_async_copy(lse_hbm, lse_ref, load_sem.at[6]),
-        pltpu.make_async_copy(o_hbm, o_ref, load_sem.at[7]),
-    ]
-    for load in kv_loads + loads:
+    early = heads // 3
+
+    def head_loads(at, count, sem):
+        on_heads = pl.ds(at, count)
+        pairs = ((q_hbm, q_ref), (do_hbm, do_ref), (o_hbm, o_ref))
+        return [pltpu.make_async_copy(src.at[on_heads], dst.at[on_heads], load_sem.at[sem + n]) for n, (src, dst) in enumerate(pairs)]
+
+    first_loads = [pltpu.make_async_copy(lse_hbm, lse_ref, load_sem.at[4])] + head_loads(0, early, 5)
+    later_loads = head_loads(early, heads - early, 8)
+    for load in kv_loads + first_loads + later_loads:
         load.start()
 
     def remote(src, dst, send, recv, target):
         return pltpu.make_async_remote_copy(src_ref=src, dst_ref=dst, send_sem=send, recv_sem=recv, device_id={'cp': target}, device_id_type=MESH)
 
-    def owner_chip(stage):
-        return jnp.where((chip == n_chips - 1) & (stage < 2), 1 - stage, stage)
+    def round_of(turn, side):
+        late, odd = turn // 2, lax.rem(turn, 2)
+        flip = jnp.where(turn == 4, side, 1 - side)
+        last_owner = jnp.where(turn == 0, 2, jnp.where(turn < 3, 1, jnp.where(turn == 3, 0, 2 * flip)))
+        last_part = jnp.where((turn == 2) | (turn >= 4), 1, 0)
+        is_last = chip == n_chips - 1
+        return jnp.where(is_last, last_owner, late), jnp.where(is_last, last_part, odd)
 
     def kv_to_chip(far, part):
         return remote(kv_ref.at[me, part], kv_ref.at[me, part], own_send.at[far, part], kv_recv.at[me, part], me + 2 * far)
@@ -64,30 +72,41 @@
     def kv_to_partner(part):
         return remote(kv_ref.at[me, part], kv_ref.at[me, part], own_send.at[0, part], kv_recv.at[me, part], partner)
 
-    def kv_forward(stage, part):
-        block = 2 * owner_chip(stage) + core
-        return remote(kv_ref.at[block, part], kv_ref.at[block, part], forward_send.at[stage, part], kv_recv.at[block, part], partner)
+    def kv_forward(owner, part):
+        block = 2 * owner + core
+        return remote(kv_ref.at[block, part], kv_ref.at[block, part], forward_send.at[owner, part], kv_recv.at[block, part], partner)
 
     def wait_kv(block, part):
         remote(kv_ref.at[block, part], kv_ref.at[block, part], own_send.at[0, part], kv_recv.at[block, part], partner).wait_recv()
 
-    def receive(stage, part):
-        wait_kv(2 * owner_chip(stage) + core, part)
-        kv_forward(stage, part).start()
+    def receive(turn):
+        owner, part = round_of(turn, core)
+        wait_kv(2 * owner + core, part)
+        kv_forward(owner, part).start()
 
     def sum_to_partner(block, slot, part):
         return remote(acc.at[block, part], from_core.at[slot, part], core_send.at[slot, part], core_recv.at[slot, part], partner)
 
-    def sum_to_owner(stage, part):
-        owner = owner_chip(stage)
+    def sum_to_owner(owner, part):
         block, slot = 2 * owner + core, chip - owner - 1
-        return remote(acc.at[block, part], from_chip.at[slot, part], chip_send.at[stage, part], chip_recv.at[slot, part], block)
-
-    def merge(stage, part):
-        block = 2 * owner_chip(stage) + core
-        sum_to_partner(block, stage, part).wait_recv()
-        acc[block, part] += from_core[stage, part]
-        sum_to_owner(stage, part).start()
+        target = jnp.where(slot == 1, 2 * (2 * n_chips - 3 - chip) + core, block)
+        return remote(acc.at[block, part], from_chip.at[slot, part], chip_send.at[owner, part], chip_recv.at[slot, part], target)
+
+    def wait_sum(slot, part):
+        remote(acc.at[me, part], from_chip.at[slot, part], chip_send.at[0, part], chip_recv.at[slot, part], partner).wait_recv()
+
+    def merge(turn):
+        owner, part = round_of(turn, core)
+        block = 2 * owner + core
+        sum_to_partner(block, owner, part).wait_recv()
+        acc[block, part] += from_core[owner, part]
+
+        @pl.when((chip >= 2) & (chip + owner == n_chips - 1))
+        def _():
+            wait_sum(1, part)
+            acc[block, part] += from_chip[1, part]
+
+        sum_to_owner(owner, part).start()
 
     def on_later_chips(action, fars):
         for far in fars:
@@ -106,18 +125,19 @@
         for part in range(2):
             kv_to_partner(part).start()
 
-    for load in loads:
+    for load in first_loads:
         load.wait()
 
-    def prepare(head, _):
-        q_t[head] = q_ref[head].T
-        do_t[head] = do_ref[head].T
-        lse_col[head] = jnp.broadcast_to(lse_ref[pl.ds(head, 1), :] * LOG2E, (dim, rows)).T
+    def prepare(head):
+        if head == early:
+            for load in later_loads:
+                load.wait()
+        at = head + me // n_dev
+        q_t[at] = q_ref[head].T
+        do_t[at] = do_ref[head].T
+        lse_col[at] = jnp.broadcast_to(lse_ref[pl.ds(at, 1), :] * LOG2E, (dim, rows)).T
         delta = jnp.sum(do_ref[head].astype(jnp.float32) * o_ref[head].astype(jnp.float32), axis=1, keepdims=True)
-        delta_col[head] = jnp.broadcast_to(delta, (rows, dim))
-        return 0
-
-    lax.fori_loop(0, heads, prepare, 0)
+        delta_col[at] = jnp.broadcast_to(delta, (rows, dim))
 
     def tile(block, part, head, slot, row_at, col_at, diagonal):
         on_rows, on_cols = slice(row_at, rows), slice(col_at, col_at + half)
@@ -156,6 +176,8 @@
         def make(head, slot):
             tile(block, 0, head, slot, 0, 0, True)
             tile(block, 1, head, slot, half, half, True)
+            if head + 1 < heads:
+                prepare(head + 1)
 
         def use(head, slot):
             add_sums(block, 0, head, slot, 0, 0)
@@ -163,18 +185,7 @@
             dq_acc[head, 0:half] = dot(s_buf[slot, 0:half, 0:half], kv_ref[block, 0, 0], NN)
             dq_acc[head, half:rows] = dot(s_buf[slot, half:rows, :], keys(block), NN)
 
-        staggered(make, use)
-
-    def full_block(block):
-        def make(head, slot):
-            tile(block, 0, head, slot, 0, 0, False)
-            tile(block, 1, head, slot, 0, half, False)
-
-        def use(head, slot):
-            add_sums(block, 0, head, slot, 0, 0)
-            add_sums(block, 1, head, slot, 0, half)
-            dq_acc[head] += dot(s_buf[slot], keys(block), NN)
-
+        prepare(0)
         staggered(make, use)
 
     def half_block(block, part):
@@ -190,23 +201,25 @@
     own_block(me)
     on_later_chips(lambda far, part: kv_to_chip(far, part).start(), [n_chips - 1])
 
-    def visit(turn, _):
-        stage, quarter = turn // 4, lax.rem(turn, 4)
-        part, odd = quarter // 2, lax.rem(quarter, 2)
-        mine = jnp.where(stage == 0, 1 - odd, odd)
-        block = 2 * owner_chip(stage) + jnp.where(mine == 1, core, 1 - core)
-
-        @pl.when((stage == 0) & (odd == 0))
-        def _():
-            receive(0, part)
-
-        @pl.when((quarter == 3) & (stage + 1 < chip))
-        def _():
-            receive(stage + 1, 0)
-
-        @pl.when((quarter == 1) & (stage >= 1))
-        def _():
-            receive(stage, 1)
+    def core_block(part):
+        wait_kv(2 * chip, part)
+        half_block(2 * chip, part)
+        sum_to_partner(2 * chip, local, part).start()
+
+    def visit(visit_id, _):
+        turn, second = visit_id // 2, lax.rem(visit_id, 2)
+        mine = jnp.where(turn < 2, 1 - second, second)
+        side = jnp.where(mine == 1, core, 1 - core)
+        owner, part = round_of(turn, side)
+        block = 2 * owner + side
+
+        @pl.when((turn < 2) & (second == 0))
+        def _():
+            receive(turn)
+
+        @pl.when((turn >= 1) & (second == 1) & (turn + 1 < 2 * chip))
+        def _():
+            receive(turn + 1)
 
         @pl.when(mine == 0)
         def _():
@@ -216,19 +229,15 @@
 
         @pl.when(mine == 0)
         def _():
-            sum_to_partner(block, stage, part).start()
-
-        @pl.when((stage == 0) & (quarter == 2))
-        def _():
-            merge(0, 0)
-
-        @pl.when(((stage == 0) & (quarter == 3) & (chip == 1)) | ((stage == 1) & (quarter == 0)))
-        def _():
-            merge(0, 1)
-
-        @pl.when((stage >= 1) & (odd == 1))
-        def _():
-            merge(stage, part)
+            sum_to_partner(block, owner, part).start()
+
+        @pl.when((turn >= 1) & (turn <= 3) & (second == 0))
+        def _():
+            merge(turn - 1)
+
+        @pl.when((second == 1) & ((turn >= 3) | ((turn == 1) & (chip == 1))))
+        def _():
+            merge(turn)
 
         return 0
 
@@ -236,11 +245,8 @@
 
     @pl.when(core == 1)
     def _():
-        for part in range(2):
-            wait_kv(2 * chip, part)
-        full_block(2 * chip)
-        for part in range(2):
-            sum_to_partner(2 * chip, local, part).start()
+        core_block(0)
+        core_block(1)
 
     for head in range(heads):
         dq_ref[head] = (dq_acc[head] * softmax_scale).astype(jnp.bfloat16)
@@ -251,13 +257,14 @@
             sum_to_partner(me, local, part).wait_recv()
         acc[me] += from_core[local]
 
-    def collect(far, part):
-        remote(acc.at[me, part], from_chip.at[far - 1, part], chip_send.at[far - 1, part], chip_recv.at[far - 1, part], partner).wait_recv()
-        acc[me, part] += from_chip[far - 1, part]
-
-    on_later_chips(collect, range(1, n_chips))
     for part in range(2):
         on_part = slice(part * half, (part + 1) * half)
+        for far in (1, n_chips - 1):
+            @pl.when(chip + far < n_chips)
+            def _():
+                wait_sum(far - 1, part)
+                acc[me, part] += from_chip[far - 1, part]
+
         dk_ref[on_part] = (acc[me, part, 0] * softmax_scale).T.astype(jnp.bfloat16)
         dv_ref[on_part] = acc[me, part, 1].T.astype(jnp.bfloat16)
 
@@ -273,11 +280,11 @@
         for part in range(2):
             sum_to_partner(2 * chip, local, part).wait_send()
 
-    def finish(stage, _):
-        for part in range(2):
-            kv_forward(stage, part).wait_send()
-            sum_to_partner(2 * owner_chip(stage) + 1 - core, stage, part).wait_send()
-            sum_to_owner(stage, part).wait_send()
+    def finish(owner, _):
+        for part in range(2):
+            kv_forward(owner, part).wait_send()
+            sum_to_partner(2 * owner + 1 - core, owner, part).wait_send()
+            sum_to_owner(owner, part).wait_send()
         return 0
 
     lax.fori_loop(0, chip, finish, 0)
@@ -330,7 +337,7 @@
                 pltpu.VMEM((2, rows, rows), bf16),
                 pltpu.VMEM((n_chips, 2, 2, dim, half), f32),
                 pltpu.VMEM((n_chips - 1, 2, 2, dim, half), f32),
-                dma((8,)),
+                dma((11,)),
                 dma((n_chips, 2)),
                 dma((n_chips - 1, 2)),
                 dma((n_dev, 2)),

time: 45.5 us -> 42.6 us (0.936)
  the two profiles are of different devices: /device:TPU:84 before, /device:TPU:81 now
where the time goes in v3:
time: 42.6 us; the launch traced here: 42.5 us
  Pallas kernels  41.8 us (98%)
  between operations  0.64 us (2%)
    pallas_call x1, Pallas kernels, local_fn(): pl.pallas_call(functools.partial(attention_kernel, n_dev, dim ** (-0.5)),...  40.8 us
    pallas_call x1, Pallas kernels, local_fn(): pl.pallas_call(store_kernel, out_shape=[jax.ShapeDtypeStruct(grad.shape,...  1.03 us

profile of v3, /device:TPU:81, one launch (start us, length us, event | category | flops | bytes accessed | tf_op | source)
XLA Modules:
  0.0 42.5 jit_solution(6431385357444406767)
XLA Ops:
  0.6 40.8 %attention_grad.1 = (bf16[7,512,128]{2,1,0:T(8,128)(2,1)S(1)}, bf16[512,128]{1,0:T(8,128)(2,1)S(1)}, bf16[512,128]{1,0:T(8,128)(2,1)S(1)}) custom-call(bf16[7,512,128]{2,1,0:T(8,128)(2,1)} %bitcast.5, bf16[512,128]{1,0:T(8,128)(2,1)} %k_hbm.1, bf16[512,128]{1,0:T(8,128)(2,1)} %v_hbm.1, bf16[7,512,128]{2,1,0:T(8,128)(2,1)} %bitcast.6, ...), custom_call_target="tpu_custom_call" | custom-call | tf_op jit(solution)/shard_map/attention_grad/pallas_call | solution.py:319
  41.4 1.0 %store_grads.1 = (bf16[7,512,128]{2,1,0:T(8,128)(2,1)}, bf16[512,128]{1,0:T(8,128)(2,1)}, bf16[512,128]{1,0:T(8,128)(2,1)}) custom-call(bf16[7,512,128]{2,1,0:T(8,128)(2,1)S(1)} %get-tuple-element.9.dq_ref, bf16[512,128]{1,0:T(8,128)(2,1)S(1)} %get-tuple-element.10.dk_ref, bf16[512,128]{1,0:T(8,128)(2,1)S(1)} %get-tuple-element.11.dv_ref), custom_call_target="tpu_custom_call" | custom-call | tf_op jit(solution)/shard_map/store_grads/pallas_call | solution.py:352

commit v4 on v3

--- a/solution.py
+++ b/solution.py
@@ -140,7 +140,7 @@
         delta_col[at] = jnp.broadcast_to(delta, (rows, dim))
 
     def tile(block, part, head, slot, row_at, col_at, diagonal):
-        on_rows, on_cols = slice(row_at, rows), slice(col_at, col_at + half)
+        on_rows, on_cols = slice(row_at, row_at + half), slice(col_at, col_at + half)
         prob = jnp.exp2(dot(q_ref[head, on_rows], kv_ref[block, part, 0], NT) * log_scale - wide(lse_col[head, on_rows], half))
         if diagonal:
             row_ids = lax.broadcasted_iota(jnp.int32, prob.shape, 0)
@@ -175,6 +175,7 @@
     def own_block(block):
         def make(head, slot):
             tile(block, 0, head, slot, 0, 0, True)
+            tile(block, 0, head, slot, half, 0, False)
             tile(block, 1, head, slot, half, half, True)
             if head + 1 < heads:
                 prepare(head + 1)
@@ -191,6 +192,7 @@
     def half_block(block, part):
         def make(head, slot):
             tile(block, part, head, slot, 0, 0, False)
+            tile(block, part, head, slot, half, 0, False)
 
         def use(head, slot):
             add_sums(block, part, head, slot, 0, 0)

time: 42.6 us -> 42.5 us (level)
  no operation moved by 1% of the time
where the time goes in v4:
time: 42.5 us; the launch traced here: 42.4 us
  Pallas kernels  41.8 us (98%)
  between operations  0.64 us (2%)
    pallas_call x1, Pallas kernels, local_fn(): pl.pallas_call(functools.partial(attention_kernel, n_dev, dim ** (-0.5)),...  40.7 us
    pallas_call x1, Pallas kernels, local_fn(): pl.pallas_call(store_kernel, out_shape=[jax.ShapeDtypeStruct(grad.shape,...  1.03 us

profile of v4, /device:TPU:81, one launch (start us, length us, event | category | flops | bytes accessed | tf_op | source)
XLA Modules:
  0.0 42.4 jit_solution(3063980671205074620)
XLA Ops:
  0.6 40.7 %attention_grad.1 = (bf16[7,512,128]{2,1,0:T(8,128)(2,1)S(1)}, bf16[512,128]{1,0:T(8,128)(2,1)S(1)}, bf16[512,128]{1,0:T(8,128)(2,1)S(1)}) custom-call(bf16[7,512,128]{2,1,0:T(8,128)(2,1)} %bitcast.5, bf16[512,128]{1,0:T(8,128)(2,1)} %k_hbm.1, bf16[512,128]{1,0:T(8,128)(2,1)} %v_hbm.1, bf16[7,512,128]{2,1,0:T(8,128)(2,1)} %bitcast.6, ...), custom_call_target="tpu_custom_call" | custom-call | tf_op jit(solution)/shard_map/attention_grad/pallas_call | solution.py:321
  41.4 1.0 %store_grads.1 = (bf16[7,512,128]{2,1,0:T(8,128)(2,1)}, bf16[512,128]{1,0:T(8,128)(2,1)}, bf16[512,128]{1,0:T(8,128)(2,1)}) custom-call(bf16[7,512,128]{2,1,0:T(8,128)(2,1)S(1)} %get-tuple-element.9.dq_ref, bf16[512,128]{1,0:T(8,128)(2,1)S(1)} %get-tuple-element.10.dk_ref, bf16[512,128]{1,0:T(8,128)(2,1)S(1)} %get-tuple-element.11.dv_ref), custom_call_target="tpu_custom_call" | custom-call | tf_op jit(solution)/shard_map/store_grads/pallas_call | solution.py:354
